TPU v7x, 32 devices: a whole 2x2x4 slice. The times are simulated.
32 devices in a mesh: tab: 8 (over y, x, core), rep: 4 (over z).
Axes of the slice: x: 2, y: 2, z: 4, core: 2. Of those that a mesh axis runs over, the one named last changes fastest.
Arguments:
- pooled: bfloat16 [64, 4096, 128], P('tab', 'rep'), may hold values from -6 to 6
- widths: int32 [64], replicated, may hold values from 16 to 128, as said below
- placement: int32 [64], replicated, may hold values from 0 to 63, each once
- route: int32 [4, 1024], P('rep'), may hold values from 0 to 1023, each once within a row
- labels: int32 [4, 1024], P('rep'), may hold values 0 or 1
- proj: bfloat16 [64, 128, 32], replicated, may hold values from -0.5 to 0.5
- senet_in: float32 [64, 32], replicated, may hold values from -6 to 6
- senet_out: float32 [32, 64], replicated, may hold values from -1 to 1
- bilinear: float32 [32, 32], replicated, may hold values from -1 to 1
- w_first: bfloat16 [4096, 256], replicated, may hold values from -0.09375 to 0.09375
- w_second: bfloat16 [256, 256], replicated, may hold values from -0.75 to 0.75
- w_last: bfloat16 [256], replicated, may hold values from -0.375 to 0.375
Outputs:
- scores: float32 [4, 1024], P('rep', 'tab')
- d_pooled: bfloat16 [64, 4096, 128], P('tab', 'rep')
- d_proj: float32 [64, 128, 32], P('tab')
- d_senet_in: float32 [64, 32], replicated
- d_senet_out: float32 [32, 64], replicated
- d_bilinear: float32 [32, 32], replicated
- d_first: float32 [4096, 256], P('tab')
- d_second: float32 [256, 256], replicated
- d_last: float32 [256], replicated
Inputs may be any that keep to these rules, and one draw needn't show every extreme that they name: `widths`: each field's width is 128, 64, 32 or 16. `placement`: a permutation of the fields. `route`: each row is a permutation of 0 to 1023.
All inputs are finite; a program needn't handle non-finite values. No bound on the sum of `labels` on one device may be relied on, other than what follows from the above.
Results may differ from a plain program's by a relative error of at most 0.017.
Values may be sent and summed in bfloat16 or wider, within the bound.
No kernel may reach another device: no remote copies, remote signals or barrier semaphores. Data moves between devices by JAX's collectives and lax.ppermute only.
A program may use at most 64 MiB of HBM per device.

v0:
```python
import jax
import jax.numpy as jnp
from jax import lax
from jax.sharding import PartitionSpec as P

PRECISE = lax.Precision.HIGHEST


def silu_slope(pre_act):
    logistic = jax.nn.sigmoid(pre_act)
    return logistic * (1.0 + pre_act * (1.0 - logistic))


def bilinear_forward(fields_in, bilinear, factor):
    product = jnp.einsum("fnc,cd->fnd", fields_in, bilinear, precision=PRECISE)
    others = jnp.sum(fields_in, axis=0, keepdims=True) - fields_in
    return (product * others * factor, product, others)


def bilinear_backward(fields_in, product, others, upstream, bilinear, factor):
    d_product = upstream * others * factor
    d_others = upstream * product * factor
    d_fields = jnp.einsum("fnd,cd->fnc", d_product, bilinear, precision=PRECISE)
    d_fields = d_fields + jnp.sum(d_others, axis=0, keepdims=True) - d_others
    d_weight = jnp.einsum("fnc,fnd->cd", fields_in, d_product, precision=PRECISE)
    return (d_fields, d_weight)


def owner_pass(embeds, targets, senet_in, senet_out, bilinear, w_first, w_second, w_last):
    count = embeds.shape[0]
    width = embeds.shape[2]
    hidden = w_second.shape[0]
    factor = count ** (-0.5)
    first = w_first.reshape(2, count, width, hidden)
    dense = embeds.astype(jnp.float32)
    squeeze = jnp.mean(dense, axis=2)
    pre_one = jnp.einsum("fn,fr->rn", squeeze, senet_in, precision=PRECISE)
    act_one = jax.nn.silu(pre_one)
    pre_two = jnp.einsum("rn,rf->fn", act_one, senet_out, precision=PRECISE)
    weights = jax.nn.sigmoid(pre_two)
    scaled = weights[:, :, None] * dense
    plain_out, plain_prod, plain_rest = bilinear_forward(dense, bilinear, factor)
    scaled_out, scaled_prod, scaled_rest = bilinear_forward(scaled, bilinear, factor)
    joined = jnp.stack([plain_out, scaled_out]).astype(jnp.bfloat16)
    pre_hidden = jnp.einsum("kfnc,kfch->nh", joined, first, preferred_element_type=jnp.float32)
    hidden_one = jax.nn.silu(pre_hidden).astype(jnp.bfloat16)
    pre_second = jnp.dot(hidden_one, w_second, preferred_element_type=jnp.float32)
    hidden_two = jax.nn.silu(pre_second).astype(jnp.bfloat16)
    logits = jnp.dot(hidden_two, w_last, preferred_element_type=jnp.float32)
    grad_logit = jax.nn.sigmoid(logits) - targets
    d_last = jnp.dot(grad_logit, hidden_two.astype(jnp.float32), precision=PRECISE)
    last_wide = w_last.astype(jnp.float32)
    d_pre_two = (grad_logit[:, None] * last_wide[None, :] * silu_slope(pre_second)).astype(
        jnp.bfloat16
    )
    d_second = jnp.dot(hidden_one.T, d_pre_two, preferred_element_type=jnp.float32)
    back_two = jnp.dot(d_pre_two, w_second.T, preferred_element_type=jnp.float32)
    d_pre_one = (back_two * silu_slope(pre_hidden)).astype(jnp.bfloat16)
    d_first = jnp.einsum(
        "kfnc,nh->kfch", joined, d_pre_one, preferred_element_type=jnp.float32
    ).reshape(-1, hidden)
    d_joined = jnp.einsum("nh,kfch->kfnc", d_pre_one, first, preferred_element_type=jnp.float32)
    d_plain, d_bil_plain = bilinear_backward(
        dense, plain_prod, plain_rest, d_joined[0], bilinear, factor
    )
    d_scaled, d_bil_scaled = bilinear_backward(
        scaled, scaled_prod, scaled_rest, d_joined[1], bilinear, factor
    )
    d_weights = jnp.sum(d_scaled * dense, axis=2)
    d_pre_w = d_weights * weights * (1.0 - weights)
    d_senet_out = jnp.einsum("rn,fn->rf", act_one, d_pre_w, precision=PRECISE)
    d_act = jnp.einsum("fn,rf->rn", d_pre_w, senet_out, precision=PRECISE) * silu_slope(pre_one)
    d_senet_in = jnp.einsum("fn,rn->fr", squeeze, d_act, precision=PRECISE)
    d_squeeze = jnp.einsum("rn,fr->fn", d_act, senet_in, precision=PRECISE)
    d_embeds = d_plain + weights[:, :, None] * d_scaled + d_squeeze[:, :, None] / width
    small = (d_senet_in, d_senet_out, d_bil_plain + d_bil_scaled, d_second, d_last)
    return (logits, d_embeds.astype(jnp.bfloat16), small, d_first, joined, d_pre_one)


def shards(
    pooled,
    widths,
    placement,
    route,
    labels,
    proj,
    senet_in,
    senet_out,
    bilinear,
    w_first,
    w_second,
    w_last,
):
    tab_count = lax.axis_size("tab")
    tab_index = lax.axis_index("tab")
    local_count = pooled.shape[0]
    rep_rows = pooled.shape[1]
    padded = pooled.shape[2]
    field_count = placement.shape[0]
    owner_rows = rep_rows // tab_count
    field_ids = jnp.arange(field_count, dtype=jnp.int32)
    matches = placement[:, None] == field_ids[None, :]
    slot_width = jnp.sum(jnp.where(matches, widths[None, :], 0), axis=1)
    slot_mask = (jnp.arange(padded, dtype=jnp.int32)[None, :] < slot_width[:, None]).astype(
        jnp.bfloat16
    )
    inverse = jnp.zeros_like(placement).at[placement].set(field_ids)
    targets = lax.dynamic_slice_in_dim(labels[0], tab_index * owner_rows, owner_rows).astype(
        jnp.float32
    )
    first_slot = tab_index * local_count
    local_fields = lax.dynamic_slice_in_dim(placement, first_slot, local_count)
    local_mask = lax.dynamic_slice_in_dim(slot_mask, first_slot, local_count, 0)
    local_proj = jnp.take(proj, local_fields, axis=0)
    masked = pooled * local_mask[:, None, :]
    embed_local = jnp.einsum(
        "fnc,fcd->fnd", masked, local_proj, preferred_element_type=jnp.float32
    ).astype(jnp.bfloat16)
    embed_slot = lax.all_to_all(embed_local, "tab", split_axis=1, concat_axis=0, tiled=True)
    logits, d_embeds, small, d_first_part, joined, d_pre_one = owner_pass(
        embed_slot[inverse], targets, senet_in, senet_out, bilinear, w_first, w_second, w_last
    )
    d_slot = d_embeds[placement]
    d_local = lax.all_to_all(d_slot, "tab", split_axis=0, concat_axis=1, tiled=True)
    back = jnp.einsum("fnd,fcd->fnc", d_local, local_proj, preferred_element_type=jnp.float32)
    back = (back * local_mask[:, None, :]).astype(jnp.bfloat16)
    d_proj_part = jnp.einsum("fnc,fnd->fcd", masked, d_local, preferred_element_type=jnp.float32)
    d_proj = lax.psum(d_proj_part.astype(jnp.bfloat16), "rep").astype(jnp.float32)
    first_all = lax.psum_scatter(d_first_part, ("tab", "rep"), scatter_dimension=0, tiled=True)
    d_first = lax.all_gather(first_all.astype(jnp.bfloat16), "rep", axis=0, tiled=True).astype(
        first_all.dtype
    )
    part_in, part_out, part_bil, part_second, part_last = small
    d_senet_in, d_senet_out, d_bilinear, d_second, d_last = lax.psum(
        (part_in, part_out, part_bil, part_second, part_last), ("tab", "rep")
    )
    all_logits = lax.all_gather(logits, "tab", axis=0, tiled=True)
    wanted = lax.dynamic_slice_in_dim(route[0], tab_index * owner_rows, owner_rows)
    scores = jnp.take(all_logits, wanted)[None, :]
    return (scores, back, d_proj, d_senet_in, d_senet_out, d_bilinear, d_first, d_second, d_last)


def solution(mesh):
    placed = (
        P("tab", "rep", None),
        P(),
        P(),
        P("rep", None),
        P("rep", None),
        P(),
        P(),
        P(),
        P(),
        P(),
        P(),
        P(),
    )
    return jax.shard_map(
        shards,
        mesh=mesh,
        in_specs=placed,
        out_specs=(
            P("rep", "tab"),
            P("tab", "rep", None),
            P("tab", None, None),
            P(),
            P(),
            P(),
            P("tab", None),
            P(),
            P(),
        ),
        check_vma=False,
    )
```

profile of v0, /device:TPU:0, one launch (start us, length us, event | category | flops | bytes accessed | tf_op | source)
XLA Modules:
  0.0 254.4 jit_solution(10931208529390182150)
XLA Ops:
  8.0 1.0 select_reduce_fusion
  9.0 0.7 compare_and_fusion
  9.9 1.6 gather_fusion
  11.5 2.4 fusion.15
  14.0 2.5 copy.54
  16.5 4.6 %reshape.143 = bf16[8,2,16384]{2,1,0:T(2,128)(2,1)} reshape(bf16[1024,8,32]{2,1,0:T(8,128)(2,1)} %bitcast.132) | data formatting | bytes 1048576
  21.0 5.2 %all-to-all-start = ((bf16[8,2,16384]{2,1,0:T(2,128)(2,1)}), bf16[8,2,16384]{2,1,0:T(2,128)(2,1)S(1)}, u32[]{:S(2)}, u32[]{:S(2)}) async-start(bf16[8,2,16384]{2,1,0:T(2,128)(2,1)} %reshape.143), calls=%async_computation | async-start | bytes 1048576 | tf_op jit(solution)/shard_map/all_to_all | solution.py:119
  26.3 1.0 scatter_custom_fusion
  27.3 8.6 %all-to-all-done = bf16[8,2,16384]{2,1,0:T(2,128)(2,1)S(1)} async-done(((bf16[8,2,16384]{2,1,0:T(2,128)(2,1)}), bf16[8,2,16384]{2,1,0:T(2,128)(2,1)S(1)}, u32[]{:S(2)}, u32[]{:S(2)}) %all-to-all-start) | async-done | bytes 524320 | tf_op jit(solution)/shard_map/all_to_all | solution.py:119
  35.9 2.0 reshape.144
  37.9 2.2 copy.56
  40.2 0.7 gather_fusion.1
  41.1 0.2 fusion.34
  41.6 1.1 fusion.9
  42.7 0.6 fusion.77
  43.3 0.4 fusion.52
  43.8 0.5 fusion.22
  44.3 0.2 copy-done.2
  44.5 0.2 copy-done.3
  44.8 0.2 multiply_convert_fusion.2
  45.0 0.8 divide_subtract_fusion
  45.9 0.2 fusion.29
  46.1 0.7 convolution_bitcast_fusion
  46.9 0.5 fusion.69
  47.4 1.5 fusion.44
  49.1 0.2 fusion.30
  49.4 1.5 fusion.14
  50.8 1.4 gather_fusion.3
  52.3 13.1 %all_to_all.36 = bf16[64,128,32]{1,2,0:T(8,128)(2,1)S(1)} all-to-all(bf16[64,128,32]{1,2,0:T(8,128)(2,1)} %gather_fusion.3), channel_id=1, replica_groups=mesh['tab'=8,'rep'=4] {'tab'}, dimensions={0} | all-to-all | bytes 1048576 | tf_op jit(solution)/shard_map/all_to_all | solution.py:124
  65.4 2.9 %fusion.25 = bf16[8,128,32]{1,2,0:T(8,128)(2,1)} fusion(bf16[8,1024,128]{2,1,0:T(8,128)(2,1)} %param.12, bf16[8,128]{1,0:T(8,128)(2,1)S(1)} %copy-done.11, bf16[8,8,4,8,128]{4,3,2,1,0:T(8,128)(2,1)S(1)} %bitcast.134), kind=kOutput, calls=%fused_computation.36 | convolution fusion | flops 71335936 | bytes 2689024 | tf_op jit(solution)/shard_map/fnc,fnd->fcd/dot_general | solution.py:127
  68.3 3.8 %fusion.107 = f32[2,64,32,256]{3,2,1,0:T(8,128)} fusion(bf16[128,256,1,1]{1,0,3,2:T(8,128)(2,1)S(1)} %fusion.29, bf16[1,64,128,32]{2,3,1,0:T(8,128)(2,1)} %copy-done.3, bf16[1,64,128,32]{2,3,1,0:T(8,128)(2,1)} %copy-done.2), kind=kOutput, calls=%fused_computation.145 | convolution fusion | flops 268959744 | bytes 5308416 | tf_op jit(solution)/shard_map/kfnc,nh->kfch/dot_general | solution.py:59
  72.2 0.7 fusion.86
  72.9 8.0 %all-gather = f32[8,1,128]{2,1,0:T(1,128)S(1)} all-gather(f32[1,1,128]{2,1,0:T(1,128)S(1)} %bitcast.137), channel_id=1, replica_groups=mesh['tab'=8,'rep'=4] {'tab'}, dimensions={0}, use_global_device_ids=true | all-gather | bytes 4608 | tf_op jit(solution)/shard_map/all_gather | solution.py:137
  80.9 1.0 gather_fusion.2
  81.9 2.0 convolution_bitcast_fusion.1
  84.0 1.2 and_select_fusion
  85.5 0.2 fusion.82
  85.7 1.0 fusion.105
  86.6 2.4 fusion.37
  89.1 41.4 %all-reduce = (f32[64,32]{0,1:T(8,128)}, f32[32,64]{1,0:T(8,128)}, f32[32,32]{1,0:T(8,128)}, f32[256]{0:T(256)}) all-reduce(f32[64,32]{0,1:T(8,128)S(1)} %fusion.71, f32[32,64]{1,0:T(8,128)S(1)} %fusion.82, f32[32,32]{1,0:T(8,128)S(1)} %fusion.37, f32[256]{0:T(256)S(1)} %bitcast.136), channel_id=1, replica_groups=mesh['tab'=8,'rep'=4] {'tab','rep'}, use_global_device_ids=true, to_apply=%region_9.10 | all-reduce | flops 5376 | bytes 43008 | tf_op jit(solution)/shard_map/psum | solution.py:134
  130.5 2.2 multiply_convert_fusion
  132.7 1.5 convert_element_type.68
  134.2 87.1 %reduce-scatter.2.cloned.1.call-done = f32[128,256]{1,0:T(8,128)} async-done(((f32[4096,256]{1,0:T(8,128)}), f32[128,256]{1,0:T(8,128)}) %reduce-scatter.2.cloned.1.call-update) | async-done | bytes 131088 | tf_op jit(solution)/shard_map/reduce_scatter | solution.py:129
  221.3 0.9 convert_element_type.69
  222.2 14.3 %all_gather.7 = bf16[512,256]{1,0:T(8,128)(2,1)S(1)} all-gather(bf16[128,256]{1,0:T(8,128)(2,1)S(1)} %convert_element_type.69), channel_id=1, replica_groups=mesh['tab'=8,'rep'=4] {'rep'}, dimensions={0}, use_global_device_ids=true | all-gather | bytes 327680 | tf_op jit(solution)/shard_map/all_gather | solution.py:130
  236.5 0.8 convert_element_type.70
  237.3 8.0 %all-reduce.6.cloned.1.call-done = f32[256,256]{1,0:T(8,128)} async-done(((f32[256,256]{1,0:T(8,128)}), f32[256,256]{1,0:T(8,128)}) %all-reduce.6.cloned.1.call-update) | async-done | bytes 262160 | tf_op jit(solution)/shard_map/psum | solution.py:134
  245.3 1.7 copy.91
  (64 shorter events, 1.5 us)
Async XLA Ops:
  8.0 35.7 %copy-start = (bf16[4096,256]{1,0:T(8,128)(2,1)S(1)}, bf16[4096,256]{1,0:T(8,128)(2,1)}, u32[]{:S(2)}) copy-start(bf16[4096,256]{1,0:T(8,128)(2,1)} %param.21) | copy-start | bytes 6291460
  9.8 6.7 %copy-start.8 = (pred[8]{0:T(512)(128)(4,1)}, pred[8]{0:T(512)(128)(4,1)S(1)}, u32[]{:S(2)}) copy-start(pred[8]{0:T(512)(128)(4,1)S(1)} %get-tuple-element.17) | copy-start | bytes 28
  9.9 6.5 %copy-start.10 = (bf16[8,128]{1,0:T(8,128)(2,1)}, bf16[8,128]{1,0:T(8,128)(2,1)S(1)}, u32[]{:S(2)}) copy-start(bf16[8,128]{1,0:T(8,128)(2,1)S(1)} %get-tuple-element.22) | copy-start | bytes 6148
  16.5 9.8 %copy-start.12 = (s32[64]{0:T(128)S(1)}, s32[64]{0:T(128)}, u32[]{:S(2)}) copy-start(s32[64]{0:T(128)} %param.14) | copy-start | bytes 772
  16.5 9.8 %copy-start.14 = (bf16[256]{0:T(256)(128)(2,1)S(1)}, bf16[256]{0:T(256)(128)(2,1)}, u32[]{:S(2)}) copy-start(bf16[256]{0:T(256)(128)(2,1)} %param.23) | copy-start | bytes 1540
  21.0 14.9 %all-to-all-start = ((bf16[8,2,16384]{2,1,0:T(2,128)(2,1)}), bf16[8,2,16384]{2,1,0:T(2,128)(2,1)S(1)}, u32[]{:S(2)}, u32[]{:S(2)}) async-start(bf16[8,2,16384]{2,1,0:T(2,128)(2,1)} %reshape.143), calls=%async_computation | async-start | bytes 1048576 | tf_op jit(solution)/shard_map/all_to_all | solution.py:119
  26.2 106.5 %all-reduce.4.cloned.1.call-start = ((), (), s32[]{:S(2)}) async-start(), calls=%async_computation.3 | async-start | bytes 131072 | tf_op jit(solution)/shard_map/psum | solution.py:128
  26.3 19.6 %copy-start.15 = (f32[256]{0:T(256)}, f32[256]{0:T(256)S(1)}, u32[]{:S(2)}) copy-start(f32[256]{0:T(256)S(1)} %convert_element_type.61) | copy-start | bytes 3076
  40.1 0.8 copy-start.5
  40.1 1.0 copy-start.6
  40.2 1.4 copy-start.4
  43.7 0.8 copy-start.2
  43.7 1.0 copy-start.3
  43.7 1.1 copy-start.13
  44.8 2.0 copy-start.17
  45.0 1.8 copy-start.19
  46.9 2.5 copy-start.1
  47.4 1.5 copy-start.7
  50.8 14.5 %copy-start.11 = (bf16[8,128]{1,0:T(8,128)(2,1)S(1)}, bf16[8,128]{1,0:T(8,128)(2,1)}, u32[]{:S(2)}) copy-start(bf16[8,128]{1,0:T(8,128)(2,1)} %copy-done.10) | copy-start | bytes 6148
  68.3 153.0 %reduce-scatter.2.cloned.1.call-start = ((), (), s32[]{:S(2)}) async-start(), calls=%async_computation.4 | async-start | bytes 4325376 | tf_op jit(solution)/shard_map/reduce_scatter | solution.py:129
  72.2 13.5 %copy-start.16 = (f32[256]{0:T(256)S(1)}, f32[256]{0:T(256)}, u32[]{:S(2)}) copy-start(f32[256]{0:T(256)} %copy-done.15) | copy-start | bytes 3076
  72.2 173.1 %all-reduce.6.cloned.1.call-start = ((), (), s32[]{:S(2)}) async-start(), calls=%async_computation.5 | async-start | bytes 524288 | tf_op jit(solution)/shard_map/psum | solution.py:134
  81.9 3.8 %copy-start.18 = (f32[128,256]{1,0:T(8,128)S(1)}, f32[128,256]{1,0:T(8,128)}, u32[]{:S(2)}) copy-start(f32[128,256]{1,0:T(8,128)} %copy-done.17) | copy-start | bytes 393220
  81.9 3.7 %copy-start.20 = (f32[128,256]{1,0:T(8,128)S(1)}, f32[128,256]{1,0:T(8,128)}, u32[]{:S(2)}) copy-start(f32[128,256]{1,0:T(8,128)} %copy-done.19) | copy-start | bytes 393220
  84.0 46.6 %copy-start.9 = (pred[8]{0:T(512)(128)(4,1)S(1)}, pred[8]{0:T(512)(128)(4,1)}, u32[]{:S(2)}) copy-start(pred[8]{0:T(512)(128)(4,1)} %copy-done.8) | copy-start | bytes 28
Sparse Core Ops, SparseCore 0:
  68.4 37.1 all-reduce.3
  111.7 133.5 all-reduce.5
Sparse Core Ops, SparseCore 1:
  72.3 149.0 reduce-scatter.1
where the time goes:
time: 255 us; the launch traced here: 254 us
  waiting for transfers between devices  104 us (41%)
  blocking collectives  76.9 us (30%)
  matrix products  25.2 us (10%)
  local copies, waits for them, and re-layouts  19.2 us (8%)
  between operations  16 us (6%)
  other arithmetic  8.18 us (3%)
  starting transfers between devices  5.32 us (2%)
    reduce_scatter x1, waiting for transfers between devices, shards(): lax.psum_scatter(d_first_part, ('tab', 'rep'), scatter_dimension=0, tiled...  87.1 us
    psum x1, blocking collectives, shards(): lax.psum((part_in, part_out, part_bil, part_second, part_last), ('tab', '...  41.4 us
    all_gather x1, blocking collectives, shards(): lax.all_gather(first_all.astype(jnp.bfloat16), 'rep', axis=0, tiled=True)  14.3 us
    all_to_all x1, blocking collectives, shards(): lax.all_to_all(d_slot, 'tab', split_axis=0, concat_axis=1, tiled=True)  13.1 us
    unnamed x46, local copies, waits for them, and re-layouts  8.85 us
    all_to_all x1, waiting for transfers between devices, shards(): lax.all_to_all(embed_local, 'tab', split_axis=1, concat_axis=0, tiled=True)  8.59 us
    all_gather x1, blocking collectives, shards(): all_logits = lax.all_gather(logits, 'tab', axis=0, tiled=True)  8.03 us
    psum x1, waiting for transfers between devices, shards(): lax.psum((part_in, part_out, part_bil, part_second, part_last), ('tab', '...  7.97 us
  transfers between devices with their start and end apart: 4, of which 3 were waited for; matrix products, arithmetic and copies ran while one was open for 7% of the time, Pallas kernels for 0%

commit v1 on v0

--- a/solution.py
+++ b/solution.py
@@ -4,6 +4,18 @@
 from jax.sharding import PartitionSpec as P
 
 PRECISE = lax.Precision.HIGHEST
+
+
+def sent_to_each(x, axis, split, join):
+    ways, here = (lax.axis_size(axis), lax.axis_index(axis))
+    width = x.shape[split] // ways
+    turned = jnp.roll(x, -here * width, axis=split)
+    got = [lax.slice_in_dim(turned, 0, width, axis=split)]
+    for far in range(1, ways):
+        sent = lax.slice_in_dim(turned, far * width, (far + 1) * width, axis=split)
+        got.append(lax.ppermute(sent, axis, [(d, (d + far) % ways) for d in range(ways)]))
+    line = jnp.concatenate(got[::-1], axis=join)
+    return jnp.roll(line, (here + 1) * got[0].shape[join], axis=join)
 
 
 def silu_slope(pre_act):
@@ -116,7 +128,7 @@
     embed_local = jnp.einsum(
         "fnc,fcd->fnd", masked, local_proj, preferred_element_type=jnp.float32
     ).astype(jnp.bfloat16)
-    embed_slot = lax.all_to_all(embed_local, "tab", split_axis=1, concat_axis=0, tiled=True)
+    embed_slot = sent_to_each(embed_local, "tab", 1, 0)
     logits, d_embeds, small, d_first_part, joined, d_pre_one = owner_pass(
         embed_slot[inverse], targets, senet_in, senet_out, bilinear, w_first, w_second, w_last
     )

time: 255 us -> 246 us (0.965)
  local copies, waits for them, and re-layouts: 19.2 us -> 8.72 us
  starting transfers between devices: 5.32 us -> 8.48 us
  waiting for transfers between devices: 104 us -> 101 us
    all_to_all x1 -> x0, waiting for transfers between devices: 8.59 us -> none  [shards(): lax.all_to_all(embed_local, 'tab', split_axis=1, concat_axis=0, tiled=True)]
    ppermute x0 -> x7, starting transfers between devices: none -> 8.36 us  [sent_to_each(): lax.ppermute(sent, axis, [(d, (d + far) % ways) for d in range(ways)])]
    ppermute x0 -> x7, waiting for transfers between devices: none -> 6.78 us  [sent_to_each(): lax.ppermute(sent, axis, [(d, (d + far) % ways) for d in range(ways)])]
    unnamed x46 -> x61, local copies, waits for them, and re-layouts: 8.85 us -> 3.07 us
    all_to_all x1 -> x0, starting transfers between devices: 5.2 us -> none  [shards(): lax.all_to_all(embed_local, 'tab', split_axis=1, concat_axis=0, tiled=True)]
  transfers between devices with their start and end apart: 4 -> 10, of which waited for: 3 -> 4; matrix products, arithmetic and copies ran while one was open for 7% -> 8% of each run, Pallas kernels for 0% -> 0%
where the time goes in v1:
time: 246 us
  waiting for transfers between devices  101 us (41%)
  blocking collectives  77.1 us (31%)
  matrix products  25.1 us (10%)
  between operations  16.1 us (7%)
  other arithmetic  9.02 us (4%)
  local copies, waits for them, and re-layouts  8.72 us (4%)
  starting transfers between devices  8.48 us (3%)
    reduce_scatter x1, waiting for transfers between devices, shards(): lax.psum_scatter(d_first_part, ('tab', 'rep'), scatter_dimension=0, tiled...  87 us
    psum x1, blocking collectives, shards(): lax.psum((part_in, part_out, part_bil, part_second, part_last), ('tab', '...  41.3 us
    all_gather x1, blocking collectives, shards(): lax.all_gather(first_all.astype(jnp.bfloat16), 'rep', axis=0, tiled=True)  14.4 us
    all_to_all x1, blocking collectives, shards(): lax.all_to_all(d_slot, 'tab', split_axis=0, concat_axis=1, tiled=True)  13.3 us
    ppermute x7, starting transfers between devices, sent_to_each(): lax.ppermute(sent, axis, [(d, (d + far) % ways) for d in range(ways)])  8.36 us
    all_gather x1, blocking collectives, shards(): all_logits = lax.all_gather(logits, 'tab', axis=0, tiled=True)  8.13 us
    psum x1, waiting for transfers between devices, shards(): lax.psum((part_in, part_out, part_bil, part_second, part_last), ('tab', '...  7.27 us
    ppermute x7, waiting for transfers between devices, sent_to_each(): lax.ppermute(sent, axis, [(d, (d + far) % ways) for d in range(ways)])  6.78 us
  transfers between devices with their start and end apart: 10, of which 4 were waited for; matrix products, arithmetic and copies ran while one was open for 8% of the time, Pallas kernels for 0%

profile of v1, /device:TPU:0, one launch (start us, length us, event | category | flops | bytes accessed | tf_op | source)
XLA Modules:
  0.0 245.6 jit_solution(17478580862682675184)
XLA Ops:
  8.1 1.0 select_reduce_fusion
  9.1 0.7 compare_and_fusion
  10.0 1.6 gather_fusion
  11.6 2.5 fusion.15
  14.1 0.3 fusion.52
  14.5 0.5 collective-permute-start.6
  15.0 2.5 %collective-permute-start.5 = (bf16[8,128,32]{1,2,0:T(8,128)(2,1)S(1)}, bf16[8,128,32]{1,2,0:T(8,128)(2,1)S(1)}, u32[]{:S(2)}, u32[]{:S(2)}) collective-permute-start(bf16[8,128,32]{1,2,0:T(8,128)(2,1)S(1)} %get-tuple-element.22), channel_id=1, source_target_pairs={{0,8},{4,12},{8,16},{12,20},{16,24},{20,28},{24,0},{28,4},{1,9},{5... | collective-permute-start | bytes 196616 | tf_op jit(solution)/shard_map/ppermute | solution.py:16
  17.6 2.4 collective-permute-start.4
  19.9 0.5 collective-permute-start.3
  20.4 0.7 collective-permute-start
  21.1 0.6 convert_element_type.61
  21.7 0.6 reshape.133
  22.3 0.8 scatter_custom_fusion
  23.1 1.0 collective-permute-start.1
  24.0 3.9 %collective-permute-done.1 = bf16[8,128,32]{1,2,0:T(8,128)(2,1)S(1)} collective-permute-done((bf16[8,128,32]{1,2,0:T(8,128)(2,1)S(1)}, bf16[8,128,32]{1,2,0:T(8,128)(2,1)S(1)}, u32[]{:S(2)}, u32[]{:S(2)}) %collective-permute-start.1) | collective-permute-done | bytes 65568 | tf_op jit(solution)/shard_map/ppermute | solution.py:16
  27.9 0.8 collective-permute-start.2
  28.7 2.9 %collective-permute-done.2 = bf16[8,128,32]{1,2,0:T(8,128)(2,1)S(1)} collective-permute-done((bf16[8,128,32]{1,2,0:T(8,128)(2,1)S(1)}, bf16[8,128,32]{1,2,0:T(8,128)(2,1)S(1)}, u32[]{:S(2)}, u32[]{:S(2)}) %collective-permute-start.2) | collective-permute-done | bytes 65568 | tf_op jit(solution)/shard_map/ppermute | solution.py:16
  32.0 0.7 gather_fusion.1
  33.0 0.2 fusion.34
  33.4 1.1 fusion.9
  34.5 0.6 fusion.78
  35.2 0.4 fusion.53
  35.6 0.5 fusion.22
  36.9 0.8 divide_subtract_fusion
  38.0 0.7 convolution_bitcast_fusion
  38.7 0.5 fusion.70
  39.3 1.5 fusion.44
  41.2 1.5 fusion.14
  42.7 1.4 gather_fusion.3
  44.1 13.3 %all_to_all.18 = bf16[64,128,32]{1,2,0:T(8,128)(2,1)S(1)} all-to-all(bf16[64,128,32]{1,2,0:T(8,128)(2,1)} %gather_fusion.3), channel_id=1, replica_groups=mesh['tab'=8,'rep'=4] {'tab'}, dimensions={0} | all-to-all | bytes 1048576 | tf_op jit(solution)/shard_map/all_to_all | solution.py:136
  57.4 2.8 %fusion.25 = bf16[8,128,32]{1,2,0:T(8,128)(2,1)} fusion(bf16[8,1024,128]{2,1,0:T(8,128)(2,1)} %param.12, bf16[8,128]{1,0:T(8,128)(2,1)S(1)} %copy-done.11, bf16[8,8,4,8,128]{4,3,2,1,0:T(8,128)(2,1)S(1)} %bitcast.126), kind=kOutput, calls=%fused_computation.36 | convolution fusion | flops 71335936 | bytes 2689024 | tf_op jit(solution)/shard_map/fnc,fnd->fcd/dot_general | solution.py:139
  60.3 3.8 %fusion.110 = f32[2,64,32,256]{3,2,1,0:T(8,128)} fusion(bf16[128,256,1,1]{1,0,3,2:T(8,128)(2,1)S(1)} %fusion.29, bf16[1,64,128,32]{2,3,1,0:T(8,128)(2,1)} %copy-done.3, bf16[1,64,128,32]{2,3,1,0:T(8,128)(2,1)} %copy-done.2), kind=kOutput, calls=%fused_computation.168 | convolution fusion | flops 268959744 | bytes 5308416 | tf_op jit(solution)/shard_map/kfnc,nh->kfch/dot_general | solution.py:71
  64.2 0.7 fusion.89
  64.9 8.1 %all-gather = f32[8,1,128]{2,1,0:T(1,128)S(1)} all-gather(f32[1,1,128]{2,1,0:T(1,128)S(1)} %bitcast.129), channel_id=1, replica_groups=mesh['tab'=8,'rep'=4] {'tab'}, dimensions={0}, use_global_device_ids=true | all-gather | bytes 4608 | tf_op jit(solution)/shard_map/all_gather | solution.py:149
  73.0 1.0 gather_fusion.2
  74.0 2.4 fusion.35
  76.5 1.2 and_select_fusion
  78.2 1.0 fusion.108
  79.1 2.0 fusion.37
  81.2 41.3 %all-reduce = (f32[64,32]{0,1:T(8,128)}, f32[32,64]{1,0:T(8,128)}, f32[32,32]{1,0:T(8,128)}, f32[256]{0:T(256)}) all-reduce(f32[64,32]{0,1:T(8,128)S(1)} %fusion.72, f32[32,64]{1,0:T(8,128)S(1)} %fusion.83, f32[32,32]{1,0:T(8,128)S(1)} %fusion.37, f32[256]{0:T(256)S(1)} %bitcast.128), channel_id=1, replica_groups=mesh['tab'=8,'rep'=4] {'tab','rep'}, use_global_device_ids=true, to_apply=%region_9.10 | all-reduce | flops 5376 | bytes 43008 | tf_op jit(solution)/shard_map/psum | solution.py:146
  122.5 2.2 multiply_convert_fusion
  124.6 1.5 convert_element_type.68
  126.2 87.0 %reduce-scatter.2.cloned.1.call-done = f32[128,256]{1,0:T(8,128)} async-done(((f32[4096,256]{1,0:T(8,128)}), f32[128,256]{1,0:T(8,128)}) %reduce-scatter.2.cloned.1.call-update) | async-done | bytes 131088 | tf_op jit(solution)/shard_map/reduce_scatter | solution.py:141
  213.2 0.9 convert_element_type.69
  214.1 14.4 %all_gather.7 = bf16[512,256]{1,0:T(8,128)(2,1)S(1)} all-gather(bf16[128,256]{1,0:T(8,128)(2,1)S(1)} %convert_element_type.69), channel_id=1, replica_groups=mesh['tab'=8,'rep'=4] {'rep'}, dimensions={0}, use_global_device_ids=true | all-gather | bytes 327680 | tf_op jit(solution)/shard_map/all_gather | solution.py:142
  228.4 0.8 convert_element_type.70
  229.3 7.3 %all-reduce.6.cloned.1.call-done = f32[256,256]{1,0:T(8,128)} async-done(((f32[256,256]{1,0:T(8,128)}), f32[256,256]{1,0:T(8,128)}) %all-reduce.6.cloned.1.call-update) | async-done | bytes 262160 | tf_op jit(solution)/shard_map/psum | solution.py:146
  236.5 1.7 copy.89
  (92 shorter events, 3.1 us)
Async XLA Ops:
  8.0 27.6 %copy-start = (bf16[4096,256]{1,0:T(8,128)(2,1)S(1)}, bf16[4096,256]{1,0:T(8,128)(2,1)}, u32[]{:S(2)}) copy-start(bf16[4096,256]{1,0:T(8,128)(2,1)} %param.21) | copy-start | bytes 6291460
  8.0 116.6 %all-reduce.4.cloned.1.call-start = ((), (), s32[]{:S(2)}) async-start(), calls=%async_computation.2 | async-start | bytes 131072 | tf_op jit(solution)/shard_map/psum | solution.py:140
  9.8 4.6 %copy-start.8 = (pred[8]{0:T(512)(128)(4,1)}, pred[8]{0:T(512)(128)(4,1)S(1)}, u32[]{:S(2)}) copy-start(pred[8]{0:T(512)(128)(4,1)S(1)} %get-tuple-element.17) | copy-start | bytes 28
  10.0 4.1 %copy-start.10 = (bf16[8,128]{1,0:T(8,128)(2,1)}, bf16[8,128]{1,0:T(8,128)(2,1)S(1)}, u32[]{:S(2)}) copy-start(bf16[8,128]{1,0:T(8,128)(2,1)S(1)} %get-tuple-element.29) | copy-start | bytes 6148
  11.6 9.5 %copy-start.13 = (s32[64]{0:T(128)S(1)}, s32[64]{0:T(128)}, u32[]{:S(2)}) copy-start(s32[64]{0:T(128)} %param.14) | copy-start | bytes 772
  11.6 9.5 %copy-start.15 = (bf16[256]{0:T(256)(128)(2,1)S(1)}, bf16[256]{0:T(256)(128)(2,1)}, u32[]{:S(2)}) copy-start(bf16[256]{0:T(256)(128)(2,1)} %param.23) | copy-start | bytes 1540
  14.5 17.2 %collective-permute-start.6 = (bf16[8,128,32]{1,2,0:T(8,128)(2,1)S(1)}, bf16[8,128,32]{1,2,0:T(8,128)(2,1)S(1)}, u32[]{:S(2)}, u32[]{:S(2)}) collective-permute-start(bf16[8,128,32]{1,2,0:T(8,128)(2,1)S(1)} %get-tuple-element.21), channel_id=1, source_target_pairs={{0,4},{4,8},{8,12},{12,16},{16,20},{20,24},{24,28},{28,0},{1,5},{5... | collective-permute-start | bytes 196616 | tf_op jit(solution)/shard_map/ppermute | solution.py:16
  15.0 16.7 %collective-permute-start.5 = (bf16[8,128,32]{1,2,0:T(8,128)(2,1)S(1)}, bf16[8,128,32]{1,2,0:T(8,128)(2,1)S(1)}, u32[]{:S(2)}, u32[]{:S(2)}) collective-permute-start(bf16[8,128,32]{1,2,0:T(8,128)(2,1)S(1)} %get-tuple-element.22), channel_id=1, source_target_pairs={{0,8},{4,12},{8,16},{12,20},{16,24},{20,28},{24,0},{28,4},{1,9},{5... | collective-permute-start | bytes 196616 | tf_op jit(solution)/shard_map/ppermute | solution.py:16
  17.6 14.1 %collective-permute-start.4 = (bf16[8,128,32]{1,2,0:T(8,128)(2,1)S(1)}, bf16[8,128,32]{1,2,0:T(8,128)(2,1)S(1)}, u32[]{:S(2)}, u32[]{:S(2)}) collective-permute-start(bf16[8,128,32]{1,2,0:T(8,128)(2,1)S(1)} %get-tuple-element.23), channel_id=1, source_target_pairs={{0,12},{4,16},{8,20},{12,24},{16,28},{20,0},{24,4},{28,8},{1,13},{... | collective-permute-start | bytes 196616 | tf_op jit(solution)/shard_map/ppermute | solution.py:16
  19.9 11.7 %collective-permute-start.3 = (bf16[8,128,32]{1,2,0:T(8,128)(2,1)S(1)}, bf16[8,128,32]{1,2,0:T(8,128)(2,1)S(1)}, u32[]{:S(2)}, u32[]{:S(2)}) collective-permute-start(bf16[8,128,32]{1,2,0:T(8,128)(2,1)S(1)} %get-tuple-element.24), channel_id=1, source_target_pairs={{0,16},{4,20},{8,24},{12,28},{16,0},{20,4},{24,8},{28,12},{1,17},{... | collective-permute-start | bytes 196616 | tf_op jit(solution)/shard_map/ppermute | solution.py:16
  20.4 2.6 %collective-permute-start = (bf16[8,128,32]{1,2,0:T(8,128)(2,1)S(1)}, bf16[8,128,32]{1,2,0:T(8,128)(2,1)S(1)}, u32[]{:S(2)}, u32[]{:S(2)}) collective-permute-start(bf16[8,128,32]{1,2,0:T(8,128)(2,1)S(1)} %get-tuple-element.27), channel_id=1, source_target_pairs={{0,28},{4,0},{8,4},{12,8},{16,12},{20,16},{24,20},{28,24},{1,29},{... | collective-permute-start | bytes 196616 | tf_op jit(solution)/shard_map/ppermute | solution.py:16
  23.1 4.8 %collective-permute-start.1 = (bf16[8,128,32]{1,2,0:T(8,128)(2,1)S(1)}, bf16[8,128,32]{1,2,0:T(8,128)(2,1)S(1)}, u32[]{:S(2)}, u32[]{:S(2)}) collective-permute-start(bf16[8,128,32]{1,2,0:T(8,128)(2,1)S(1)} %get-tuple-element.26), channel_id=1, source_target_pairs={{0,24},{4,28},{8,0},{12,4},{16,8},{20,12},{24,16},{28,20},{1,25},{... | collective-permute-start | bytes 196616 | tf_op jit(solution)/shard_map/ppermute | solution.py:16
  27.9 3.7 %collective-permute-start.2 = (bf16[8,128,32]{1,2,0:T(8,128)(2,1)S(1)}, bf16[8,128,32]{1,2,0:T(8,128)(2,1)S(1)}, u32[]{:S(2)}, u32[]{:S(2)}) collective-permute-start(bf16[8,128,32]{1,2,0:T(8,128)(2,1)S(1)} %get-tuple-element.25), channel_id=1, source_target_pairs={{0,20},{4,24},{8,28},{12,0},{16,4},{20,8},{24,12},{28,16},{1,21},{... | collective-permute-start | bytes 196616 | tf_op jit(solution)/shard_map/ppermute | solution.py:16
  32.0 0.8 copy-start.5
  32.0 1.0 copy-start.6
  32.0 1.4 copy-start.4
  35.6 0.8 copy-start.2
  35.6 1.0 copy-start.3
  35.6 1.1 copy-start.14
  35.6 1.3 copy-start.12
  35.6 2.1 copy-start.16
  36.7 2.0 copy-start.18
  36.9 1.8 copy-start.20
  38.7 2.5 %copy-start.1 = (f32[2,64,128,32]{2,3,1,0:T(8,128)}, f32[2,64,128,32]{2,3,1,0:T(8,128)S(1)}, u32[]{:S(2)}) copy-start(f32[2,64,128,32]{2,3,1,0:T(8,128)S(1)} %convolution_bitcast_fusion) | copy-start | bytes 6291460
  39.2 1.5 copy-start.7
  42.7 14.7 %copy-start.11 = (bf16[8,128]{1,0:T(8,128)(2,1)S(1)}, bf16[8,128]{1,0:T(8,128)(2,1)}, u32[]{:S(2)}) copy-start(bf16[8,128]{1,0:T(8,128)(2,1)} %copy-done.10) | copy-start | bytes 6148
  60.2 152.9 %reduce-scatter.2.cloned.1.call-start = ((), (), s32[]{:S(2)}) async-start(), calls=%async_computation.3 | async-start | bytes 4325376 | tf_op jit(solution)/shard_map/reduce_scatter | solution.py:141
  64.2 14.0 %copy-start.17 = (f32[256]{0:T(256)S(1)}, f32[256]{0:T(256)}, u32[]{:S(2)}) copy-start(f32[256]{0:T(256)} %convert_element_type.61) | copy-start | bytes 3076
  64.2 172.4 %all-reduce.6.cloned.1.call-start = ((), (), s32[]{:S(2)}) async-start(), calls=%async_computation.4 | async-start | bytes 524288 | tf_op jit(solution)/shard_map/psum | solution.py:146
  74.0 4.2 %copy-start.19 = (f32[128,256]{1,0:T(8,128)S(1)}, f32[128,256]{1,0:T(8,128)}, u32[]{:S(2)}) copy-start(f32[128,256]{1,0:T(8,128)} %copy-done.18) | copy-start | bytes 393220
  74.0 4.2 %copy-start.21 = (f32[128,256]{1,0:T(8,128)S(1)}, f32[128,256]{1,0:T(8,128)}, u32[]{:S(2)}) copy-start(f32[128,256]{1,0:T(8,128)} %copy-done.20) | copy-start | bytes 393220
  76.5 46.0 %copy-start.9 = (pred[8]{0:T(512)(128)(4,1)S(1)}, pred[8]{0:T(512)(128)(4,1)}, u32[]{:S(2)}) copy-start(pred[8]{0:T(512)(128)(4,1)} %copy-done.8) | copy-start | bytes 28
Sparse Core Ops, SparseCore 0:
  60.4 37.3 all-reduce.3
  103.9 132.6 all-reduce.5
Sparse Core Ops, SparseCore 1:
  64.2 148.9 reduce-scatter.1
